TPU v7x, 256 devices: a whole 4x4x8 slice. The times are simulated.
256 devices in a mesh: span: 256 (over y, x, z, core).
Axes of the slice: x: 4, y: 4, z: 8, core: 2. Of those that a mesh axis runs over, the one named last changes fastest.
Arguments:
- returns: bfloat16 [256, 2097152], P(None, 'span'), may hold values from -40 to 40
- market: bfloat16 [2097152], P('span'), may hold values from -12 to 12
- mask: int32 [2097152], P('span'), may hold values 0 or 1
- counts: int32 [256], P('span'), may hold values from 0 to 8192, as said below
Outputs:
- slope: float32 [256, 1048576], P(None, 'span')
Inputs may be any that keep to these rules, and one draw needn't show every extreme that they name: For every span d, the counts of spans 0 to d sum to between (d + 1) * 4096 and (d + 2) * 4096; all counts sum to exactly 1048576; some span holds exactly 8192.
All inputs are finite; a program needn't handle non-finite values. No bound on the sum of `mask` on one device may be relied on, other than what follows from the above.
Results may differ from a plain program's by a relative error of at most 0.00039.
Values may be sent and summed in bfloat16 or wider, within the bound.
A program may use at most 64 MiB of HBM per device.

v0:
```python
import jax
import jax.numpy as jnp
from jax import lax
from jax.sharding import Mesh
from jax.sharding import PartitionSpec as P

WIN = 1024
BLOCK = 512
QROWS = 4096
SPAN = ("span_0", "span_1", "span_2", "span_3")
RIDGE = 0.1


def in_order(parts, dim):
    parts = jnp.moveaxis(parts, 0, dim)
    dims = parts.shape
    return parts.reshape(*dims[:dim], dims[dim] * dims[dim + 1], *dims[dim + 2 :])


def stacked_from(x, axes, sequence):
    parts = x[None]
    for k in sequence:
        parts = lax.all_gather(parts, axes[k], axis=0, tiled=True)
    block = [lax.axis_size(axes[k]) for k in reversed(sequence)]
    parts = parts.reshape(*block, *x.shape)
    turned = sorted(range(len(sequence)), key=lambda place: sequence[len(sequence) - 1 - place])
    return parts.transpose(*turned, *range(len(sequence), parts.ndim)).reshape(-1, *x.shape)


def whole_of(x, axes, sequence, dim):
    return in_order(stacked_from(x, axes, sequence), dim)


def shifted(value, axis, steps):
    count = lax.axis_size(axis)
    initial, last = (max(0, -steps), min(count, count - steps))
    return lax.ppermute(value, axis, [(source, source + steps) for source in range(initial, last)])


def band_matrix():
    row_index = jnp.arange(BLOCK + WIN, dtype=jnp.int32)[:, None]
    col_index = jnp.arange(BLOCK, dtype=jnp.int32)[None, :]
    inside = (row_index >= col_index + 1) & (row_index <= col_index + WIN)
    return inside.astype(jnp.bfloat16)


def stacked(y_values, x_values, w_values):
    cross_terms = (x_values.astype(jnp.float32)[None, :] * y_values.astype(jnp.float32)).astype(
        jnp.bfloat16
    )
    square = (x_values.astype(jnp.float32) * x_values.astype(jnp.float32)).astype(jnp.bfloat16)
    return jnp.concatenate(
        [cross_terms, y_values, w_values[None, :], x_values[None, :], square[None, :]], 0
    )


def slopes_of(moments):
    stocks = (moments.shape[0] - 3) // 2
    sum_xy = moments[:stocks]
    sum_y = moments[stocks : 2 * stocks]
    sum_w = moments[2 * stocks]
    sum_x = moments[2 * stocks + 1]
    sum_xx = moments[2 * stocks + 2]
    numerator = sum_w * sum_xy - sum_x * sum_y
    denominator = sum_w * sum_xx - sum_x * sum_x + RIDGE * WIN * WIN
    return numerator / denominator


def per_device(returns, market, mask, counts):
    quota = QROWS
    my_index = lax.axis_index(SPAN)
    own_count = counts[0]
    gathered = whole_of(counts, (("span_0", "span_1", "span_2"), "span_3"), (0, 1), 0)
    earlier = jnp.arange(gathered.shape[0], dtype=jnp.int32) < my_index
    before = jnp.sum(jnp.where(earlier, gathered, 0))
    capacity = returns.shape[1]
    row_index = jnp.arange(capacity, dtype=jnp.int32)
    weight = jnp.where(row_index < own_count, mask, 0).astype(jnp.float32)
    y_values = (returns.astype(jnp.float32) * weight[None, :]).astype(jnp.bfloat16)
    x_values = (market.astype(jnp.float32) * weight).astype(jnp.bfloat16)
    combined = jnp.concatenate(
        [y_values, x_values[None, :], weight.astype(jnp.bfloat16)[None, :]], 0
    )
    padded = jnp.pad(combined, ((0, 0), (quota, 0)))
    shift_base = my_index * quota - before

    def take_rows(first, length):
        return lax.dynamic_slice_in_dim(padded, first + quota, length, 1)

    own_rows = take_rows(shift_base, quota)
    near_piece = shifted(take_rows(shift_base + quota - WIN, quota + WIN), SPAN, 1)
    far_piece = shifted(take_rows(shift_base + 2 * quota - WIN, WIN), SPAN, 2)
    halo_rows = near_piece[:, :WIN] + far_piece
    window = own_rows + near_piece[:, WIN:]
    extended = jnp.concatenate([halo_rows, window], 1)
    stocks = extended.shape[0] - 2
    stacked_rows = stacked(extended[:stocks], extended[stocks], extended[stocks + 1])
    band_ones = band_matrix()

    def one_block(block_index):
        window_piece = lax.dynamic_slice_in_dim(stacked_rows, block_index * BLOCK, BLOCK + WIN, 1)
        return slopes_of(jnp.dot(window_piece, band_ones, preferred_element_type=jnp.float32))

    blocks = lax.map(one_block, jnp.arange(quota // BLOCK, dtype=jnp.int32))
    return jnp.transpose(blocks, (1, 0, 2)).reshape(stocks, quota)


def solution(mesh):
    finer = Mesh(mesh.devices.reshape(4, 4, 8, 2), ("span_0", "span_1", "span_2", "span_3"))
    return jax.shard_map(
        per_device,
        mesh=finer,
        in_specs=(P(None, SPAN), P(SPAN), P(SPAN), P(SPAN)),
        out_specs=P(None, SPAN),
        check_vma=False,
    )
```

profile of v0, /device:TPU:9, one launch (start us, length us, event | category | flops | bytes accessed | tf_op | source)
XLA Modules:
  0.0 168.3 jit_solution(13319208394564157042)
XLA Ops:
  0.7 1.3 dynamic-slice
  2.7 23.9 %all-reduce.1 = s32[128]{0:T(128)S(1)} all-reduce(s32[128]{0:T(128)S(1)} %dynamic-update-slice), channel_id=2, replica_groups=mesh['span_0'=4,'span_1'=4,'span_2'=8,'span_3'=2] {'span_0','span_1','sp..., use_global_device_ids=true, to_apply=%add.1 | all-reduce | flops 128 | bytes 1024
  26.6 8.1 %all-gather.2 = s32[2,1,128]{2,1,0:T(1,128)S(1)} all-gather(s32[1,1,128]{2,1,0:T(1,128)S(1)} %bitcast.34), channel_id=3, replica_groups=mesh['span_0'=4,'span_1'=4,'span_2'=8,'span_3'=2] {'span_3'}, dimensions={0}, use_global_device_ids=true | all-gather | bytes 1536 | tf_op jit(solution)/shard_map/all_gather | solution.py:23
  36.7 5.2 %multiply_convert_fusion = bf16[256,8192]{1,0:T(8,128)(2,1)} fusion(bf16[256,8192]{1,0:T(8,128)(2,1)} %param.6, f32[8192]{0:T(1024)S(1)} %get-tuple-element.66), kind=kLoop, calls=%fused_computation.23 | loop fusion | flops 6291456 | bytes 8421376 | tf_op jit(solution)/shard_map/convert_element_type | solution.py:79
  41.9 3.9 %fusion.20 = bf16[258,12288]{1,0:T(8,128)(2,1)S(1)} fusion(bf16[1,8192]{1,0:T(2,128)(2,1)S(1)} %broadcast_in_dim.33, bf16[1,8192]{1,0:T(2,128)(2,1)S(1)} %broadcast_in_dim.32, bf16[256,8192]{1,0:T(8,128)(2,1)} %multiply_convert_fusion), kind=kLoop, calls=%fused_computation.25 | loop fusion | flops 31703040 | bytes 10567680 | tf_op jit(solution)/shard_map/concatenate | solution.py:81
  45.8 2.7 %copy-done = bf16[258,12288]{1,0:T(8,128)(2,1)} copy-done((bf16[258,12288]{1,0:T(8,128)(2,1)}, bf16[258,12288]{1,0:T(8,128)(2,1)S(1)}, u32[]{:S(2)}) %copy-start) | copy-done | bytes 6340632
  48.5 2.6 %constant_dynamic-slice_fusion.1 = bf16[258,5120]{1,0:T(8,128)(2,1)} fusion(bf16[258,12288]{1,0:T(8,128)(2,1)S(1)} %fusion.20, s32[]{:T(128)S(6)} %select_n.23), kind=kLoop, calls=%fused_computation.43 | loop fusion | bytes 5283844 | tf_op jit(solution)/shard_map/dynamic_slice | solution.py:88
  51.1 2.9 %collective-permute-start = (bf16[258,5120]{1,0:T(8,128)(2,1)}, bf16[258,5120]{1,0:T(8,128)(2,1)S(1)}, u32[]{:S(2)}, u32[]{:S(2)}) collective-permute-start(bf16[258,5120]{1,0:T(8,128)(2,1)} %constant_dynamic-slice_fusion.1), channel_id=1, source_target_pairs={{0,1},{1,2},{2,3},{3,4},{4,5},{5,6},{6,7},{7,8},{8,9},{9,10},{10,1... | collective-permute-start | bytes 7925768 | tf_op jit(solution)/shard_map/ppermute | solution.py:37
  54.0 2.1 %constant_dynamic-slice_fusion = bf16[258,1024]{1,0:T(8,128)(2,1)} fusion(bf16[258,12288]{1,0:T(8,128)(2,1)} %copy-done, s32[]{:T(128)S(6)} %select_n.24), kind=kLoop, calls=%fused_computation.42 | loop fusion | bytes 1056772 | tf_op jit(solution)/shard_map/dynamic_slice | solution.py:88
  56.1 2.6 %collective-permute-start.1 = (bf16[258,1024]{1,0:T(8,128)(2,1)}, bf16[258,1024]{1,0:T(8,128)(2,1)S(1)}, u32[]{:S(2)}, u32[]{:S(2)}) collective-permute-start(bf16[258,1024]{1,0:T(8,128)(2,1)} %constant_dynamic-slice_fusion), channel_id=1, source_target_pairs={{0,2},{1,3},{2,4},{3,5},{4,6},{5,7},{6,8},{7,9},{8,10},{9,11},{10,... | collective-permute-start | bytes 1585160 | tf_op jit(solution)/shard_map/ppermute | solution.py:37
  58.8 41.9 %collective-permute-done.1 = bf16[258,1024]{1,0:T(8,128)(2,1)S(1)} collective-permute-done((bf16[258,1024]{1,0:T(8,128)(2,1)}, bf16[258,1024]{1,0:T(8,128)(2,1)S(1)}, u32[]{:S(2)}, u32[]{:S(2)}) %collective-permute-start.1) | collective-permute-done | bytes 528416 | tf_op jit(solution)/shard_map/ppermute | solution.py:37
  100.7 2.8 %slice_add_fusion = bf16[258,4096]{1,0:T(8,128)(2,1)S(1)} fusion(bf16[258,5120]{1,0:T(8,128)(2,1)S(1)} %collective-permute-done, bf16[258,12288]{1,0:T(8,128)(2,1)} %copy-done, s32[]{:T(128)S(6)} %select_n.25), kind=kLoop, calls=%fused_computation.30 | loop fusion | flops 4227072 | bytes 6340612 | tf_op jit(solution)/shard_map/add | solution.py:94
  103.7 2.0 %multiply_convert_fusion.1 = (bf16[256,5120]{1,0:T(8,128)(2,1)S(1)}, bf16[256,5120]{1,0:T(8,128)(2,1)}) fusion(f32[5120]{0:T(1024)S(1)} %bitcast.32, bf16[258,4096]{1,0:T(8,128)(2,1)S(1)} %slice_add_fusion, bf16[258,1024]{1,0:T(8,128)(2,1)S(1)} %slice_add_fusion.1), kind=kLoop, calls=%fused_computation.26 | loop fusion | flops 9175040 | bytes 7905280 | tf_op jit(solution)/shard_map/convert_element_type | solution.py:48
  105.7 19.2 %concatenate.11 = bf16[515,5120]{1,0:T(8,128)(2,1)} concatenate(bf16[256,5120]{1,0:T(8,128)(2,1)S(1)} %get-tuple-element.63, bf16[256,5120]{1,0:T(8,128)(2,1)} %get-tuple-element.64, bf16[1,5120]{1,0:T(2,128)(2,1)S(1)} %pad_maximum_fusion, bf16[1,5120]{1,0:T(2,128)(2,1)S(1)} %get-tuple-element.62, bf16[1,5120]{1,0:T(2,128)(2,1)S(1)} %get-tuple-element.61), dimensions={0} | concatenate | bytes 10547200 | tf_op jit(solution)/shard_map/concatenate | solution.py:52
  124.9 38.6 %while.11 = (s32[]{:T(128)}, f32[8,256,512]{2,1,0:T(8,128)}, s32[8]{0:T(128)S(1)}, bf16[515,5120]{1,0:T(8,128)(2,1)}, s32[512]{0:T(512)S(1)}, /*index=5*/s32[512...) while((s32[]{:T(128)}, f32[8,256,512]{2,1,0:T(8,128)}, s32[8]{0:T(128)S(1)}, ...), condition=%wide.region_2.3_spmd.clone, body=%wide.region_1.2_spmd.clone.sunk | while | flops 813697024 | bytes 4248227 | solution.py:104
  126.1 2.6 %fusion.32 = f32[515,512]{1,0:T(8,128)S(1)} fusion(bf16[515,5120]{1,0:T(8,128)(2,1)} %get-tuple-element.138, s32[]{:T(128)S(6)} %select_n.33, s32[512]{0:T(512)S(1)} %get-tuple-element.140, s32[512]{0:T(512)S(1)} %get-tuple-element.139), kind=kOutput, calls=%fused_computation.5.clone.1 | convolution fusion | flops 813170688 | bytes 2656260 | tf_op jit(solution)/shard_map/while/body/eval_jaxpr/dot_general | solution.py:102
  131.0 2.6 %fusion.32 = f32[515,512]{1,0:T(8,128)S(1)} fusion(bf16[515,5120]{1,0:T(8,128)(2,1)} %get-tuple-element.138, s32[]{:T(128)S(6)} %select_n.33, s32[512]{0:T(512)S(1)} %get-tuple-element.140, s32[512]{0:T(512)S(1)} %get-tuple-element.139), kind=kOutput, calls=%fused_computation.5.clone.1 | convolution fusion | flops 813170688 | bytes 2656260 | tf_op jit(solution)/shard_map/while/body/eval_jaxpr/dot_general | solution.py:102
  135.8 2.6 %fusion.32 = f32[515,512]{1,0:T(8,128)S(1)} fusion(bf16[515,5120]{1,0:T(8,128)(2,1)} %get-tuple-element.138, s32[]{:T(128)S(6)} %select_n.33, s32[512]{0:T(512)S(1)} %get-tuple-element.140, s32[512]{0:T(512)S(1)} %get-tuple-element.139), kind=kOutput, calls=%fused_computation.5.clone.1 | convolution fusion | flops 813170688 | bytes 2656260 | tf_op jit(solution)/shard_map/while/body/eval_jaxpr/dot_general | solution.py:102
  140.6 2.6 %fusion.32 = f32[515,512]{1,0:T(8,128)S(1)} fusion(bf16[515,5120]{1,0:T(8,128)(2,1)} %get-tuple-element.138, s32[]{:T(128)S(6)} %select_n.33, s32[512]{0:T(512)S(1)} %get-tuple-element.140, s32[512]{0:T(512)S(1)} %get-tuple-element.139), kind=kOutput, calls=%fused_computation.5.clone.1 | convolution fusion | flops 813170688 | bytes 2656260 | tf_op jit(solution)/shard_map/while/body/eval_jaxpr/dot_general | solution.py:102
  145.4 2.6 %fusion.32 = f32[515,512]{1,0:T(8,128)S(1)} fusion(bf16[515,5120]{1,0:T(8,128)(2,1)} %get-tuple-element.138, s32[]{:T(128)S(6)} %select_n.33, s32[512]{0:T(512)S(1)} %get-tuple-element.140, s32[512]{0:T(512)S(1)} %get-tuple-element.139), kind=kOutput, calls=%fused_computation.5.clone.1 | convolution fusion | flops 813170688 | bytes 2656260 | tf_op jit(solution)/shard_map/while/body/eval_jaxpr/dot_general | solution.py:102
  150.2 2.6 %fusion.32 = f32[515,512]{1,0:T(8,128)S(1)} fusion(bf16[515,5120]{1,0:T(8,128)(2,1)} %get-tuple-element.138, s32[]{:T(128)S(6)} %select_n.33, s32[512]{0:T(512)S(1)} %get-tuple-element.140, s32[512]{0:T(512)S(1)} %get-tuple-element.139), kind=kOutput, calls=%fused_computation.5.clone.1 | convolution fusion | flops 813170688 | bytes 2656260 | tf_op jit(solution)/shard_map/while/body/eval_jaxpr/dot_general | solution.py:102
  155.1 2.6 %fusion.32 = f32[515,512]{1,0:T(8,128)S(1)} fusion(bf16[515,5120]{1,0:T(8,128)(2,1)} %get-tuple-element.138, s32[]{:T(128)S(6)} %select_n.33, s32[512]{0:T(512)S(1)} %get-tuple-element.140, s32[512]{0:T(512)S(1)} %get-tuple-element.139), kind=kOutput, calls=%fused_computation.5.clone.1 | convolution fusion | flops 813170688 | bytes 2656260 | tf_op jit(solution)/shard_map/while/body/eval_jaxpr/dot_general | solution.py:102
  159.9 2.6 %fusion.32 = f32[515,512]{1,0:T(8,128)S(1)} fusion(bf16[515,5120]{1,0:T(8,128)(2,1)} %get-tuple-element.138, s32[]{:T(128)S(6)} %select_n.33, s32[512]{0:T(512)S(1)} %get-tuple-element.140, s32[512]{0:T(512)S(1)} %get-tuple-element.139), kind=kOutput, calls=%fused_computation.5.clone.1 | convolution fusion | flops 813170688 | bytes 2656260 | tf_op jit(solution)/shard_map/while/body/eval_jaxpr/dot_general | solution.py:102
  163.5 4.8 %copy.7 = f32[8,32,8,512]{3,2,0,1:T(8,128)} copy(f32[8,32,8,512]{3,2,1,0:T(8,128)} %bitcast.13) | data formatting | bytes 8388608 | tf_op jit(solution)/shard_map/reshape | solution.py:105
  (40 shorter events, 14.6 us)
Async XLA Ops:
  45.8 2.7 %copy-start = (bf16[258,12288]{1,0:T(8,128)(2,1)}, bf16[258,12288]{1,0:T(8,128)(2,1)S(1)}, u32[]{:S(2)}) copy-start(bf16[258,12288]{1,0:T(8,128)(2,1)S(1)} %fusion.20) | copy-start | bytes 19021828
  51.1 49.5 %collective-permute-start = (bf16[258,5120]{1,0:T(8,128)(2,1)}, bf16[258,5120]{1,0:T(8,128)(2,1)S(1)}, u32[]{:S(2)}, u32[]{:S(2)}) collective-permute-start(bf16[258,5120]{1,0:T(8,128)(2,1)} %constant_dynamic-slice_fusion.1), channel_id=1, source_target_pairs={{0,1},{1,2},{2,3},{3,4},{4,5},{5,6},{6,7},{7,8},{8,9},{9,10},{10,1... | collective-permute-start | bytes 7925768 | tf_op jit(solution)/shard_map/ppermute | solution.py:37
  56.1 44.5 %collective-permute-start.1 = (bf16[258,1024]{1,0:T(8,128)(2,1)}, bf16[258,1024]{1,0:T(8,128)(2,1)S(1)}, u32[]{:S(2)}, u32[]{:S(2)}) collective-permute-start(bf16[258,1024]{1,0:T(8,128)(2,1)} %constant_dynamic-slice_fusion), channel_id=1, source_target_pairs={{0,2},{1,3},{2,4},{3,5},{4,6},{5,7},{6,8},{7,9},{8,10},{9,11},{10,... | collective-permute-start | bytes 1585160 | tf_op jit(solution)/shard_map/ppermute | solution.py:37
where the time goes:
time: 169 us; the launch traced here: 168 us
  waiting for transfers between devices  41.9 us (25%)
  local copies, waits for them, and re-layouts  38.2 us (23%)
  blocking collectives  31.9 us (19%)
  other arithmetic  23.1 us (14%)
  matrix products  21 us (12%)
  starting transfers between devices  5.48 us (3%)
  loops' own time  5.37 us (3%)
    ppermute x2, waiting for transfers between devices, shifted(): lax.ppermute(value, axis, [(source, source + steps) for source in range(i...  41.9 us
    unnamed x1, blocking collectives  23.9 us
    dot_general x8, matrix products, one_block(): jnp.dot(window_piece, band_ones, preferred_element_type=jnp.float32)  21 us
    concatenate x1, local copies, waits for them, and re-layouts, stacked(): jnp.concatenate([cross_terms, y_values, w_values[None, :], x_values[None,...  19.2 us
    all_gather x1, blocking collectives, stacked_from(): parts = lax.all_gather(parts, axes[k], axis=0, tiled=True)  8.07 us
    dynamic_update_slice x8, other arithmetic, per_device(): blocks = lax.map(one_block, jnp.arange(quota // BLOCK, dtype=jnp.int32))  7.47 us
    ppermute x2, starting transfers between devices, shifted(): lax.ppermute(value, axis, [(source, source + steps) for source in range(i...  5.48 us
    another operation x1, loops' own time, per_device(): blocks = lax.map(one_block, jnp.arange(quota // BLOCK, dtype=jnp.int32))  5.37 us
  transfers between devices with their start and end apart: 2, of which 1 were waited for; matrix products, arithmetic and copies ran while one was open for 1% of the time, Pallas kernels for 0%

commit v1 on v0

--- a/solution.py
+++ b/solution.py
@@ -20,7 +20,9 @@
 def stacked_from(x, axes, sequence):
     parts = x[None]
     for k in sequence:
-        parts = lax.all_gather(parts, axes[k], axis=0, tiled=True)
+        parts = jnp.concatenate(
+            lax.all_to_all(jnp.stack([parts] * lax.axis_size(axes[k])), axes[k], 0, 0), axis=0
+        )
     block = [lax.axis_size(axes[k]) for k in reversed(sequence)]
     parts = parts.reshape(*block, *x.shape)
     turned = sorted(range(len(sequence)), key=lambda place: sequence[len(sequence) - 1 - place])

time: 169 us -> 158 us (0.935)
  blocking collectives: 31.9 us -> 5.46 us
  starting transfers between devices: 5.48 us -> 19.7 us
  local copies, waits for them, and re-layouts: 38.2 us -> 35.9 us
    unnamed x1 -> x0, blocking collectives: 23.9 us -> none
    all_to_all x0 -> x1, starting transfers between devices: none -> 14.9 us  [stacked_from(): lax.all_to_all(jnp.stack([parts] * lax.axis_size(axes[k])), axes[k], 0, 0)]
    all_gather x1 -> x0, blocking collectives: 8.07 us -> none  [stacked_from(): parts = lax.all_gather(parts, axes[k], axis=0, tiled=True)]
    all_to_all x0 -> x1, blocking collectives: none -> 5.46 us  [stacked_from(): lax.all_to_all(jnp.stack([parts] * lax.axis_size(axes[k])), axes[k], 0, 0)]
    unnamed x5 -> x0, local copies, waits for them, and re-layouts: 4.72 us -> none
    all_to_all x0 -> x1, other arithmetic: none -> 2.35 us  [stacked_from(): lax.all_to_all(jnp.stack([parts] * lax.axis_size(axes[k])), axes[k], 0, 0)]
    convert_element_type x1, other arithmetic: 5.16 us -> 3.35 us  [per_device(): (returns.astype(jnp.float32) * weight[None, :]).astype(jnp.bfloat16)]
    dynamic_slice x2, local copies, waits for them, and re-layouts: 4.72 us -> 6.48 us  [take_rows(): return lax.dynamic_slice_in_dim(padded, first + quota, length, 1)]
  transfers between devices with their start and end apart: 2 -> 3, of which waited for: 1 -> 2; matrix products, arithmetic and copies ran while one was open for 1% -> 7% of each run, Pallas kernels for 0% -> 0%
where the time goes in v1:
time: 158 us; the launch traced here: 157 us
  waiting for transfers between devices  43.3 us (27%)
  local copies, waits for them, and re-layouts  35.9 us (23%)
  other arithmetic  24.7 us (16%)
  matrix products  21 us (13%)
  starting transfers between devices  19.7 us (12%)
  blocking collectives  5.46 us (3%)
  loops' own time  5.37 us (3%)
    ppermute x2, waiting for transfers between devices, shifted(): lax.ppermute(value, axis, [(source, source + steps) for source in range(i...  42.5 us
    dot_general x8, matrix products, one_block(): jnp.dot(window_piece, band_ones, preferred_element_type=jnp.float32)  21 us
    concatenate x1, local copies, waits for them, and re-layouts, stacked(): jnp.concatenate([cross_terms, y_values, w_values[None, :], x_values[None,...  19.2 us
    all_to_all x1, starting transfers between devices, stacked_from(): lax.all_to_all(jnp.stack([parts] * lax.axis_size(axes[k])), axes[k], 0, 0)  14.9 us
    dynamic_update_slice x8, other arithmetic, per_device(): blocks = lax.map(one_block, jnp.arange(quota // BLOCK, dtype=jnp.int32))  7.51 us
    dynamic_slice x2, local copies, waits for them, and re-layouts, take_rows(): return lax.dynamic_slice_in_dim(padded, first + quota, length, 1)  6.48 us
    all_to_all x1, blocking collectives, stacked_from(): lax.all_to_all(jnp.stack([parts] * lax.axis_size(axes[k])), axes[k], 0, 0)  5.46 us
    another operation x1, loops' own time, per_device(): blocks = lax.map(one_block, jnp.arange(quota // BLOCK, dtype=jnp.int32))  5.37 us
  transfers between devices with their start and end apart: 3, of which 2 were waited for; matrix products, arithmetic and copies ran while one was open for 7% of the time, Pallas kernels for 0%

profile of v1, /device:TPU:9, one launch (start us, length us, event | category | flops | bytes accessed | tf_op | source)
XLA Modules:
  0.0 156.8 jit_solution(16957464072776374625)
XLA Ops:
  1.3 14.9 %all-to-all-start = ((s32[128,1,1]{2,1,0:T(1,128)}), s32[128,1,1]{2,1,0:T(1,128)S(1)}, u32[]{:S(2)}, u32[]{:S(2)}) async-start(s32[128,1,1]{2,1,0:T(1,128)} %stack.6), calls=%async_computation | async-start | bytes 131072 | tf_op jit(solution)/shard_map/all_to_all | solution.py:24
  17.0 3.3 %multiply_convert_fusion = bf16[256,8192]{1,0:T(8,128)(2,1)S(1)} fusion(bf16[256,8192]{1,0:T(8,128)(2,1)} %param.6, f32[8192]{0:T(1024)S(1)} %get-tuple-element.66), kind=kLoop, calls=%fused_computation.23 | loop fusion | flops 6291456 | bytes 8421376 | tf_op jit(solution)/shard_map/convert_element_type | solution.py:81
  20.4 5.0 %fusion.20 = bf16[258,12288]{1,0:T(8,128)(2,1)} fusion(bf16[1,8192]{1,0:T(2,128)(2,1)S(1)} %broadcast_in_dim.30, bf16[1,8192]{1,0:T(2,128)(2,1)S(1)} %broadcast_in_dim.29, bf16[256,8192]{1,0:T(8,128)(2,1)S(1)} %multiply_convert_fusion), kind=kLoop, calls=%fused_computation.25 | loop fusion | flops 31703040 | bytes 10567680 | tf_op jit(solution)/shard_map/concatenate | solution.py:83
  26.1 2.3 %reduce.1 = s32[128]{0:T(128)S(1)} reduce(s32[128,1,1]{2,1,0:T(1,128)S(1)} %all-to-all-done, s32[]{:T(128)} %constant.52.clone.1), dimensions={1,2}, to_apply=%all_to_all.6.reduce_sub_computation | reduce | bytes 1028 | tf_op jit(solution)/shard_map/all_to_all | solution.py:24
  28.5 5.5 %all_to_all.10 = s32[2,128,1]{1,2,0:T(1,128)S(1)} all-to-all(s32[2,128,1]{1,2,0:T(1,128)S(1)} %pad_add_fusion), channel_id=1, replica_groups=mesh['span_0'=4,'span_1'=4,'span_2'=8,'span_3'=2] {'span_3'}, dimensions={0} | all-to-all | bytes 2048 | tf_op jit(solution)/shard_map/all_to_all | solution.py:24
  35.3 4.4 %constant_dynamic-slice_fusion.1 = bf16[258,5120]{1,0:T(8,128)(2,1)} fusion(bf16[258,12288]{1,0:T(8,128)(2,1)} %fusion.20, s32[]{:T(128)S(6)} %select_n.23), kind=kLoop, calls=%fused_computation.44 | loop fusion | bytes 5283844 | tf_op jit(solution)/shard_map/dynamic_slice | solution.py:90
  39.6 2.5 %collective-permute-start = (bf16[258,5120]{1,0:T(8,128)(2,1)}, bf16[258,5120]{1,0:T(8,128)(2,1)S(1)}, u32[]{:S(2)}, u32[]{:S(2)}) collective-permute-start(bf16[258,5120]{1,0:T(8,128)(2,1)} %constant_dynamic-slice_fusion.1), channel_id=1, source_target_pairs={{0,1},{1,2},{2,3},{3,4},{4,5},{5,6},{6,7},{7,8},{8,9},{9,10},{10,1... | collective-permute-start | bytes 7925768 | tf_op jit(solution)/shard_map/ppermute | solution.py:39
  42.1 2.1 %constant_dynamic-slice_fusion = bf16[258,1024]{1,0:T(8,128)(2,1)} fusion(bf16[258,12288]{1,0:T(8,128)(2,1)} %fusion.20, s32[]{:T(128)S(6)} %select_n.24), kind=kLoop, calls=%fused_computation.43 | loop fusion | bytes 1056772 | tf_op jit(solution)/shard_map/dynamic_slice | solution.py:90
  44.2 2.3 %collective-permute-start.1 = (bf16[258,1024]{1,0:T(8,128)(2,1)}, bf16[258,1024]{1,0:T(8,128)(2,1)S(1)}, u32[]{:S(2)}, u32[]{:S(2)}) collective-permute-start(bf16[258,1024]{1,0:T(8,128)(2,1)} %constant_dynamic-slice_fusion), channel_id=1, source_target_pairs={{0,2},{1,3},{2,4},{3,5},{4,6},{5,7},{6,8},{7,9},{8,10},{9,11},{10,... | collective-permute-start | bytes 1585160 | tf_op jit(solution)/shard_map/ppermute | solution.py:39
  46.6 42.5 %collective-permute-done.1 = bf16[258,1024]{1,0:T(8,128)(2,1)S(1)} collective-permute-done((bf16[258,1024]{1,0:T(8,128)(2,1)}, bf16[258,1024]{1,0:T(8,128)(2,1)S(1)}, u32[]{:S(2)}, u32[]{:S(2)}) %collective-permute-start.1) | collective-permute-done | bytes 528416 | tf_op jit(solution)/shard_map/ppermute | solution.py:39
  89.2 2.8 %slice_add_fusion = bf16[258,4096]{1,0:T(8,128)(2,1)S(1)} fusion(bf16[258,5120]{1,0:T(8,128)(2,1)S(1)} %collective-permute-done, bf16[258,12288]{1,0:T(8,128)(2,1)} %fusion.20, s32[]{:T(128)S(6)} %select_n.25), kind=kLoop, calls=%fused_computation.30 | loop fusion | flops 4227072 | bytes 6340612 | tf_op jit(solution)/shard_map/add | solution.py:96
  92.1 2.0 %multiply_convert_fusion.1 = (bf16[256,5120]{1,0:T(8,128)(2,1)S(1)}, bf16[256,5120]{1,0:T(8,128)(2,1)}) fusion(f32[5120]{0:T(1024)S(1)} %bitcast.33, bf16[258,4096]{1,0:T(8,128)(2,1)S(1)} %slice_add_fusion, bf16[258,1024]{1,0:T(8,128)(2,1)S(1)} %slice_add_fusion.1), kind=kLoop, calls=%fused_computation.26 | loop fusion | flops 9175040 | bytes 7905280 | tf_op jit(solution)/shard_map/convert_element_type | solution.py:50
  94.2 19.2 %concatenate.11 = bf16[515,5120]{1,0:T(8,128)(2,1)} concatenate(bf16[256,5120]{1,0:T(8,128)(2,1)S(1)} %get-tuple-element.63, bf16[256,5120]{1,0:T(8,128)(2,1)} %get-tuple-element.64, bf16[1,5120]{1,0:T(2,128)(2,1)S(1)} %pad_maximum_fusion, bf16[1,5120]{1,0:T(2,128)(2,1)S(1)} %get-tuple-element.62, bf16[1,5120]{1,0:T(2,128)(2,1)S(1)} %get-tuple-element.61), dimensions={0} | concatenate | bytes 10547200 | tf_op jit(solution)/shard_map/concatenate | solution.py:54
  113.4 38.6 %while.11 = (s32[]{:T(128)}, f32[8,256,512]{2,1,0:T(8,128)}, s32[8]{0:T(128)S(1)}, bf16[515,5120]{1,0:T(8,128)(2,1)}, s32[512]{0:T(512)S(1)}, /*index=5*/s32[512...) while((s32[]{:T(128)}, f32[8,256,512]{2,1,0:T(8,128)}, s32[8]{0:T(128)S(1)}, ...), condition=%wide.region_2.3_spmd.clone, body=%wide.region_1.2_spmd.clone.sunk | while | flops 813697024 | bytes 4248227 | solution.py:106
  114.6 2.6 %fusion.32 = f32[515,512]{1,0:T(8,128)S(1)} fusion(bf16[515,5120]{1,0:T(8,128)(2,1)} %get-tuple-element.138, s32[]{:T(128)S(6)} %select_n.33, s32[512]{0:T(512)S(1)} %get-tuple-element.140, s32[512]{0:T(512)S(1)} %get-tuple-element.139), kind=kOutput, calls=%fused_computation.5.clone.1 | convolution fusion | flops 813170688 | bytes 2656260 | tf_op jit(solution)/shard_map/while/body/eval_jaxpr/dot_general | solution.py:104
  119.4 2.6 %fusion.32 = f32[515,512]{1,0:T(8,128)S(1)} fusion(bf16[515,5120]{1,0:T(8,128)(2,1)} %get-tuple-element.138, s32[]{:T(128)S(6)} %select_n.33, s32[512]{0:T(512)S(1)} %get-tuple-element.140, s32[512]{0:T(512)S(1)} %get-tuple-element.139), kind=kOutput, calls=%fused_computation.5.clone.1 | convolution fusion | flops 813170688 | bytes 2656260 | tf_op jit(solution)/shard_map/while/body/eval_jaxpr/dot_general | solution.py:104
  124.2 2.6 %fusion.32 = f32[515,512]{1,0:T(8,128)S(1)} fusion(bf16[515,5120]{1,0:T(8,128)(2,1)} %get-tuple-element.138, s32[]{:T(128)S(6)} %select_n.33, s32[512]{0:T(512)S(1)} %get-tuple-element.140, s32[512]{0:T(512)S(1)} %get-tuple-element.139), kind=kOutput, calls=%fused_computation.5.clone.1 | convolution fusion | flops 813170688 | bytes 2656260 | tf_op jit(solution)/shard_map/while/body/eval_jaxpr/dot_general | solution.py:104
  129.0 2.6 %fusion.32 = f32[515,512]{1,0:T(8,128)S(1)} fusion(bf16[515,5120]{1,0:T(8,128)(2,1)} %get-tuple-element.138, s32[]{:T(128)S(6)} %select_n.33, s32[512]{0:T(512)S(1)} %get-tuple-element.140, s32[512]{0:T(512)S(1)} %get-tuple-element.139), kind=kOutput, calls=%fused_computation.5.clone.1 | convolution fusion | flops 813170688 | bytes 2656260 | tf_op jit(solution)/shard_map/while/body/eval_jaxpr/dot_general | solution.py:104
  131.7 1.0 fusion.34
  133.9 2.6 %fusion.32 = f32[515,512]{1,0:T(8,128)S(1)} fusion(bf16[515,5120]{1,0:T(8,128)(2,1)} %get-tuple-element.138, s32[]{:T(128)S(6)} %select_n.33, s32[512]{0:T(512)S(1)} %get-tuple-element.140, s32[512]{0:T(512)S(1)} %get-tuple-element.139), kind=kOutput, calls=%fused_computation.5.clone.1 | convolution fusion | flops 813170688 | bytes 2656260 | tf_op jit(solution)/shard_map/while/body/eval_jaxpr/dot_general | solution.py:104
  138.7 2.6 %fusion.32 = f32[515,512]{1,0:T(8,128)S(1)} fusion(bf16[515,5120]{1,0:T(8,128)(2,1)} %get-tuple-element.138, s32[]{:T(128)S(6)} %select_n.33, s32[512]{0:T(512)S(1)} %get-tuple-element.140, s32[512]{0:T(512)S(1)} %get-tuple-element.139), kind=kOutput, calls=%fused_computation.5.clone.1 | convolution fusion | flops 813170688 | bytes 2656260 | tf_op jit(solution)/shard_map/while/body/eval_jaxpr/dot_general | solution.py:104
  143.5 2.6 %fusion.32 = f32[515,512]{1,0:T(8,128)S(1)} fusion(bf16[515,5120]{1,0:T(8,128)(2,1)} %get-tuple-element.138, s32[]{:T(128)S(6)} %select_n.33, s32[512]{0:T(512)S(1)} %get-tuple-element.140, s32[512]{0:T(512)S(1)} %get-tuple-element.139), kind=kOutput, calls=%fused_computation.5.clone.1 | convolution fusion | flops 813170688 | bytes 2656260 | tf_op jit(solution)/shard_map/while/body/eval_jaxpr/dot_general | solution.py:104
  148.4 2.6 %fusion.32 = f32[515,512]{1,0:T(8,128)S(1)} fusion(bf16[515,5120]{1,0:T(8,128)(2,1)} %get-tuple-element.138, s32[]{:T(128)S(6)} %select_n.33, s32[512]{0:T(512)S(1)} %get-tuple-element.140, s32[512]{0:T(512)S(1)} %get-tuple-element.139), kind=kOutput, calls=%fused_computation.5.clone.1 | convolution fusion | flops 813170688 | bytes 2656260 | tf_op jit(solution)/shard_map/while/body/eval_jaxpr/dot_general | solution.py:104
  151.9 4.8 %copy.8 = f32[8,32,8,512]{3,2,0,1:T(8,128)} copy(f32[8,32,8,512]{3,2,1,0:T(8,128)} %bitcast.10) | data formatting | bytes 8388608 | tf_op jit(solution)/shard_map/reshape | solution.py:107
  (39 shorter events, 14.3 us)
Async XLA Ops:
  1.3 24.8 %all-to-all-start = ((s32[128,1,1]{2,1,0:T(1,128)}), s32[128,1,1]{2,1,0:T(1,128)S(1)}, u32[]{:S(2)}, u32[]{:S(2)}) async-start(s32[128,1,1]{2,1,0:T(1,128)} %stack.6), calls=%async_computation | async-start | bytes 131072 | tf_op jit(solution)/shard_map/all_to_all | solution.py:24
  39.6 49.5 %collective-permute-start = (bf16[258,5120]{1,0:T(8,128)(2,1)}, bf16[258,5120]{1,0:T(8,128)(2,1)S(1)}, u32[]{:S(2)}, u32[]{:S(2)}) collective-permute-start(bf16[258,5120]{1,0:T(8,128)(2,1)} %constant_dynamic-slice_fusion.1), channel_id=1, source_target_pairs={{0,1},{1,2},{2,3},{3,4},{4,5},{5,6},{6,7},{7,8},{8,9},{9,10},{10,1... | collective-permute-start | bytes 7925768 | tf_op jit(solution)/shard_map/ppermute | solution.py:39
  44.2 44.9 %collective-permute-start.1 = (bf16[258,1024]{1,0:T(8,128)(2,1)}, bf16[258,1024]{1,0:T(8,128)(2,1)S(1)}, u32[]{:S(2)}, u32[]{:S(2)}) collective-permute-start(bf16[258,1024]{1,0:T(8,128)(2,1)} %constant_dynamic-slice_fusion), channel_id=1, source_target_pairs={{0,2},{1,3},{2,4},{3,5},{4,6},{5,7},{6,8},{7,9},{8,10},{9,11},{10,... | collective-permute-start | bytes 1585160 | tf_op jit(solution)/shard_map/ppermute | solution.py:39
